TPU v7x, 32 devices: a whole 2x2x4 slice. The times are simulated.
32 devices in a mesh: dp: 2 (over x), tp: 4 (over z), section: 4 (over y, core).
Axes of the slice: x: 2, y: 2, z: 4, core: 2. Of those that a mesh axis runs over, the one named last changes fastest.
Arguments:
- tokens: bfloat16 [256, 2304], P('dp', 'section'), may hold values from -6 to 6
- hidden_grad: bfloat16 [256, 18432], P('dp', ('tp', 'section')), may hold values from -6 to 6
- norm_gain: float32 [2304], replicated, may hold values from 0.5 to 1.5
- w_gate: bfloat16 [2304, 18432], P('dp', ('tp', 'section')), may hold values from -0.125 to 0.125
- w_up: bfloat16 [2304, 18432], P('dp', ('tp', 'section')), may hold values from -0.125 to 0.125
Outputs:
- grad_tokens: bfloat16 [256, 2304], P('dp', ('tp', 'section'))
- grad_gain: float32 [2304], P(('tp', 'section'))
- grad_gate: bfloat16 [2304, 18432], P('dp', ('tp', 'section'))
- grad_up: bfloat16 [2304, 18432], P('dp', ('tp', 'section'))
All inputs are finite; a program needn't handle non-finite values.
Results may differ from a plain program's by a relative error of at most 0.018.
Values may be sent and summed in bfloat16 or wider, within the bound.
A program may use at most 128 MiB of HBM per device.

v0:
```python
import jax
import jax.numpy as jnp
from jax import lax
from jax.sharding import PartitionSpec as P

D = 2304
epsilon = 1e-06


def gated_unit(gate, up):
    return jax.nn.gelu(gate, approximate=True) * up


def shards(tokens, hidden_grad, norm_gain, w_gate, w_up):
    rows_in = lax.all_gather(tokens, "section", axis=1, tiled=True)
    inputs = rows_in.astype(jnp.float32)
    inv_rms = lax.rsqrt(jnp.mean(inputs * inputs, axis=1) + epsilon)
    normed = (inputs * inv_rms[:, None] * norm_gain).astype(jnp.bfloat16)
    full_gate, full_up = (
        lax.all_gather(w_gate, "dp", axis=0, tiled=True),
        lax.all_gather(w_up, "dp", axis=0, tiled=True),
    )
    gate = jnp.dot(normed, full_gate, preferred_element_type=jnp.float32)
    up = jnp.dot(normed, full_up, preferred_element_type=jnp.float32)
    hidden, pull = jax.vjp(gated_unit, gate, up)
    d_gate, d_up = pull(hidden_grad.astype(jnp.float32))
    d_gate = d_gate.astype(jnp.bfloat16)
    d_up = d_up.astype(jnp.bfloat16)
    contract_cols = (((1,), (1,)), ((), ()))
    contract_rows = (((0,), (0,)), ((), ()))
    features = full_gate.shape[0]
    own_width = features // lax.axis_size(("tp", "section"))
    first = lax.dot_general(full_gate, d_gate, contract_cols, preferred_element_type=jnp.float32)
    second = lax.dot_general(full_up, d_up, contract_cols, preferred_element_type=jnp.float32)
    d_columns = lax.psum_scatter(
        (first + second).astype(jnp.bfloat16), ("tp", "section"), scatter_dimension=0, tiled=True
    ).astype(jnp.float32)
    d_normed = d_columns.T
    offset = lax.axis_index(("tp", "section")) * own_width
    own_inputs = lax.dynamic_slice_in_dim(inputs, offset, own_width, 1)
    own_gain = lax.dynamic_slice_in_dim(norm_gain, offset, own_width, 0)
    gain_part = jnp.sum(d_normed * own_inputs * inv_rms[:, None], axis=0)
    row_part = jnp.sum(own_inputs * own_gain * d_normed, axis=1)
    grad_gain = lax.psum(gain_part, "dp")
    row_sum = lax.psum(row_part, ("tp", "section"))
    grad_tokens = (
        inv_rms[:, None] * own_gain * d_normed - own_inputs * (inv_rms**3 * row_sum / D)[:, None]
    )
    block = w_gate.shape[0]
    fwidth = w_gate.shape[1]
    cols_normed = lax.all_to_all(normed, "dp", split_axis=1, concat_axis=0, tiled=True)
    per_device = normed.shape[0]
    empty = jnp.zeros((block, fwidth), jnp.float32)
    piece_gate = lax.all_gather(d_gate, "dp", axis=0, tiled=True)
    piece_up = lax.all_gather(d_up, "dp", axis=0, tiled=True)

    def one_block(index, running):
        inner = index * per_device
        block_normed = lax.dynamic_slice_in_dim(cols_normed, inner, per_device, 0)
        block_gate = lax.dynamic_slice_in_dim(piece_gate, inner, per_device, 0)
        block_up = lax.dynamic_slice_in_dim(piece_up, inner, per_device, 0)
        terms = (
            lax.dot_general(
                block_normed, block_gate, contract_rows, preferred_element_type=jnp.float32
            ),
            lax.dot_general(
                block_normed, block_up, contract_rows, preferred_element_type=jnp.float32
            ),
        )
        return tuple(
            (
                total + lax.optimization_barrier(term.astype(jnp.bfloat16)).astype(jnp.float32)
                for total, term in zip(running, terms)
            )
        )

    sum_gate, sum_up = lax.fori_loop(
        0, piece_gate.shape[0] // per_device, one_block, (empty, empty)
    )
    return (
        grad_tokens.astype(jnp.bfloat16),
        grad_gain,
        sum_gate.astype(jnp.bfloat16),
        sum_up.astype(jnp.bfloat16),
    )


def solution(mesh):
    in_specs = (
        P("dp", "section"),
        P("dp", ("tp", "section")),
        P(),
        P("dp", ("tp", "section")),
        P("dp", ("tp", "section")),
    )
    out_specs = (
        P("dp", ("tp", "section")),
        P(("tp", "section")),
        P("dp", ("tp", "section")),
        P("dp", ("tp", "section")),
    )
    return jax.shard_map(shards, mesh=mesh, in_specs=in_specs, out_specs=out_specs, check_vma=False)
```

profile of v0, /device:TPU:0, one launch (start us, length us, event | category | flops | bytes accessed | tf_op | source)
XLA Modules:
  0.0 266.3 jit_solution(6498756828406113752)
XLA Ops:
  7.2 0.0 copy-start.3
  7.2 0.0 copy-start.4
  7.2 0.0 all-gather.5.cloned.1.call-start
  7.2 0.7 all-gather.5.cloned.1.call-update
  7.9 0.0 copy-start.2
  7.9 0.0 all-gather.3.cloned.1.call-start
  8.0 0.7 all-gather.3.cloned.1.call-update
  8.7 0.0 copy-done.3
  8.7 9.0 %all_gather.15 = bf16[128,2304]{0,1:T(8,128)(2,1)S(1)} all-gather(bf16[128,576]{0,1:T(8,128)(2,1)S(1)} %copy-done.3), channel_id=1, replica_groups=mesh['dp'=2,'tp'=4,'section'=4] {'section'}, dimensions={1}, use_global_device_ids=true | all-gather | bytes 737280 | tf_op jit(solution)/shard_map/all_gather | solution.py:15
  17.7 0.3 multiply_reduce_fusion
  18.1 0.0 copy-done.4
  18.1 0.4 multiply_convert_fusion
  18.4 1.1 copy.13
  19.5 3.5 %all-to-all-start = ((bf16[128,2,1152]{2,0,1:T(8,128)(2,1)}), bf16[128,2,1152]{2,0,1:T(8,128)(2,1)S(1)}, u32[]{:S(2)}, u32[]{:S(2)}) async-start(bf16[128,2,1152]{2,0,1:T(8,128)(2,1)} %copy.13), calls=%async_computation | async-start | bytes 1179648 | tf_op jit(solution)/shard_map/all_to_all | solution.py:51
  23.0 0.0 reduce-scatter.4.cloned.1.call-start
  23.1 1.1 convert_element_type.59
  24.2 0.1 dynamic_slice.27
  24.3 63.6 %all-gather.5.cloned.1.call-done = bf16[2304,1152]{1,0:T(8,128)(2,1)} async-done(((bf16[1152,1152]{1,0:T(8,128)(2,1)}), bf16[2304,1152]{1,0:T(8,128)(2,1)}) %all-gather.5.cloned.1.call-update) | async-done | bytes 5308432 | tf_op jit(solution)/shard_map/all_gather | solution.py:20
  87.9 0.0 copy-done.2
  87.9 3.7 %fusion.8 = (bf16[128,1152]{1,0:T(8,128)(2,1)S(1)}, f32[128,1152]{1,0:T(8,128)S(1)}) fusion(bf16[128,1152]{1,0:T(8,128)(2,1)S(1)} %copy-done.2, bf16[128,2304]{0,1:T(8,128)(2,1)S(1)} %multiply_convert_fusion, bf16[2304,1152]{1,0:T(8,128)(2,1)} %all-gather.5.cloned.1.call-done), kind=kOutput, calls=%fused_computation.19 | convolution fusion | flops 681099264 | bytes 7077888 | tf_op jit(solution)/shard_map/dot_general | solution.py:23
  91.6 67.1 %all-gather.3.cloned.1.call-done = bf16[2304,1152]{1,0:T(8,128)(2,1)} async-done(((bf16[1152,1152]{1,0:T(8,128)(2,1)}), bf16[2304,1152]{1,0:T(8,128)(2,1)}) %all-gather.3.cloned.1.call-update) | async-done | bytes 5308432 | tf_op jit(solution)/shard_map/all_gather | solution.py:21
  158.7 4.0 %fusion.15 = bf16[128,1152]{1,0:T(8,128)(2,1)S(1)} fusion(f32[128,1152]{1,0:T(8,128)S(1)} %get-tuple-element.158, bf16[128,2304]{0,1:T(8,128)(2,1)S(1)} %multiply_convert_fusion, bf16[2304,1152]{1,0:T(8,128)(2,1)} %all-gather.3.cloned.1.call-done, bf16[128,1152]{1,0:T(8,128)(2,1)} %param.8), kind=kOutput, calls=%fused_computation.26 | convolution fusion | flops 682721280 | bytes 7077888 | tf_op jit(solution)/shard_map/dot_general | solution.py:24
  162.7 0.0 slice-done
  162.7 0.0 slice-done.1
  162.7 0.0 copy-start.1
  162.7 1.6 fusion.23
  164.3 0.9 copy-done.1
  165.2 1.6 fusion.7
  166.8 1.1 copy.14
  167.9 0.0 reduce-scatter.4.cloned.1.call-update
  167.9 9.3 %all_gather.19 = bf16[256,1152]{1,0:T(8,128)(2,1)} all-gather(bf16[128,1152]{1,0:T(8,128)(2,1)S(1)} %get-tuple-element.157), channel_id=1, replica_groups=mesh['dp'=2,'tp'=4,'section'=4] {'dp'}, dimensions={0}, use_global_device_ids=true | all-gather | bytes 884736 | tf_op jit(solution)/shard_map/all_gather | solution.py:55
  177.2 8.5 %all_gather.18 = bf16[256,1152]{1,0:T(8,128)(2,1)} all-gather(bf16[128,1152]{1,0:T(8,128)(2,1)S(1)} %fusion.15), channel_id=1, replica_groups=mesh['dp'=2,'tp'=4,'section'=4] {'dp'}, dimensions={0}, use_global_device_ids=true | all-gather | bytes 884736 | tf_op jit(solution)/shard_map/all_gather | solution.py:54
  185.7 0.0 all-to-all-done
  185.7 27.0 %while.16 = (s32[]{:T(128)}, f32[1152,1152]{1,0:T(8,128)}, f32[1152,1152]{1,0:T(8,128)}, bf16[256,1152]{1,0:T(8,128)(2,1)S(1)}, bf16[256,1152]{1,0:T(8,128)(2,1)...) while((s32[]{:T(128)}, f32[1152,1152]{1,0:T(8,128)}, ...), condition=%wide.region_7.0_spmd.clone, body=%wide.region_6.0_spmd.clone.sunk | while | flops 690094080 | bytes 33032356 | solution.py:77
  185.7 1.8 convolution_convert_fusion.4
  187.6 3.4 %convolution_convert_fusion.5 = bf16[1152,1152]{1,0:T(8,128)(2,1)} fusion(bf16[256,1152]{1,0:T(8,128)(2,1)} %get-tuple-element.224, s32[]{:T(128)S(6)} %select_n.16, bf16[256,1152]{1,0:T(8,128)(2,1)S(1)} %get-tuple-element.223), kind=kOutput, calls=%fused_computation.1.clone.1 | convolution fusion | flops 341065728 | bytes 3245056 | tf_op jit(solution)/shard_map/while/body/eval_jaxpr/dot_general | solution.py:63
  190.9 6.7 %select_add_fusion.3 = (f32[1152,1152]{1,0:T(8,128)}, f32[1152,1152]{1,0:T(8,128)}) fusion(f32[1152,1152]{1,0:T(8,128)} %get-tuple-element.212, bf16[1152,1152]{1,0:T(8,128)(2,1)S(1)} %convolution_convert_fusion.4, pred[]{:T(512)S(6)} %compare.3, bf16[1152,1152]{1,0:T(8,128)(2,1)} %convolution_convert_fusion.5, f32[1152,1152]{1,0:T(8,128)} %get-tuple-element.211), kind=kLoop, calls=%fused_computation.2.clone.1 | loop fusion | flops 7962624 | bytes 26542080 | tf_op jit(solution)/shard_map/while/body/eval_jaxpr/add | solution.py:72
  197.6 1.8 convolution_convert_fusion.4
  199.5 3.4 %convolution_convert_fusion.5 = bf16[1152,1152]{1,0:T(8,128)(2,1)} fusion(bf16[256,1152]{1,0:T(8,128)(2,1)} %get-tuple-element.224, s32[]{:T(128)S(6)} %select_n.16, bf16[256,1152]{1,0:T(8,128)(2,1)S(1)} %get-tuple-element.223), kind=kOutput, calls=%fused_computation.1.clone.1 | convolution fusion | flops 341065728 | bytes 3245056 | tf_op jit(solution)/shard_map/while/body/eval_jaxpr/dot_general | solution.py:63
  202.8 9.9 %select_add_fusion.3 = (f32[1152,1152]{1,0:T(8,128)}, f32[1152,1152]{1,0:T(8,128)}) fusion(f32[1152,1152]{1,0:T(8,128)} %get-tuple-element.212, bf16[1152,1152]{1,0:T(8,128)(2,1)S(1)} %convolution_convert_fusion.4, pred[]{:T(512)S(6)} %compare.3, bf16[1152,1152]{1,0:T(8,128)(2,1)} %convolution_convert_fusion.5, f32[1152,1152]{1,0:T(8,128)} %get-tuple-element.211), kind=kLoop, calls=%fused_computation.2.clone.1 | loop fusion | flops 7962624 | bytes 26542080 | tf_op jit(solution)/shard_map/while/body/eval_jaxpr/add | solution.py:72
  212.7 4.4 %convert_element_type.68 = bf16[1152,1152]{1,0:T(8,128)(2,1)} convert(f32[1152,1152]{1,0:T(8,128)} %get-tuple-element.115) | non-fusion elementwise | flops 1327104 | bytes 7962624 | tf_op jit(solution)/shard_map/convert_element_type | solution.py:84
  217.1 0.2 copy-done
  217.3 1.8 convert_element_type.67
  219.1 3.0 %reduce-scatter.4.cloned.1.call-done = bf16[144,128]{1,0:T(8,128)(2,1)} async-done(((bf16[2304,128]{1,0:T(8,128)(2,1)}), bf16[144,128]{1,0:T(8,128)(2,1)}) %reduce-scatter.4.cloned.1.call-update) | async-done | bytes 36880 | tf_op jit(solution)/shard_map/reduce_scatter | solution.py:35
  222.1 1.1 fusion.20
  223.2 5.5 %psum.15 = f32[144]{0:T(256)} all-reduce(f32[144]{0:T(256)S(1)} %get-tuple-element.141), channel_id=1, replica_groups=mesh['dp'=2,'tp'=4,'section'=4] {'dp'}, use_global_device_ids=true, to_apply=%region_5.0 | all-reduce | flops 144 | bytes 1152 | tf_op jit(solution)/shard_map/psum | solution.py:44
  228.6 29.5 %psum.14 = f32[128]{0:T(128)S(1)} all-reduce(f32[128]{0:T(128)S(1)} %get-tuple-element.142), channel_id=1, replica_groups=mesh['dp'=2,'tp'=4,'section'=4] {'tp','section'}, use_global_device_ids=true, to_apply=%region_3.0 | all-reduce | flops 128 | bytes 1024 | tf_op jit(solution)/shard_map/psum | solution.py:45
  258.1 1.6 fusion.17
  (8 shorter events, 0.0 us)
Async XLA Ops:
  7.2 1.5 copy-start.3
  7.2 10.9 %copy-start.4 = (f32[2304]{0:T(1024)S(1)}, f32[2304]{0:T(1024)}, u32[]{:S(2)}) copy-start(f32[2304]{0:T(1024)} %param.9) | copy-start | bytes 27652
  7.2 80.7 %all-gather.5.cloned.1.call-start = ((), (), s32[]{:S(2)}) async-start(), calls=%async_computation.3 | async-start | bytes 7962624 | tf_op jit(solution)/shard_map/all_gather | solution.py:20
  7.9 80.0 %copy-start.2 = (bf16[128,1152]{1,0:T(8,128)(2,1)S(1)}, bf16[128,1152]{1,0:T(8,128)(2,1)}, u32[]{:S(2)}) copy-start(bf16[128,1152]{1,0:T(8,128)(2,1)} %param.8) | copy-start | bytes 884740
  7.9 150.8 %all-gather.3.cloned.1.call-start = ((), (), s32[]{:S(2)}) async-start(), calls=%async_computation.2 | async-start | bytes 7962624 | tf_op jit(solution)/shard_map/all_gather | solution.py:21
  19.5 166.2 %all-to-all-start = ((bf16[128,2,1152]{2,0,1:T(8,128)(2,1)}), bf16[128,2,1152]{2,0,1:T(8,128)(2,1)S(1)}, u32[]{:S(2)}, u32[]{:S(2)}) async-start(bf16[128,2,1152]{2,0,1:T(8,128)(2,1)} %copy.13), calls=%async_computation | async-start | bytes 1179648 | tf_op jit(solution)/shard_map/all_to_all | solution.py:51
  23.0 199.1 %reduce-scatter.4.cloned.1.call-start = ((), (), s32[]{:S(2)}) async-start(), calls=%async_computation.4 | async-start | bytes 626688 | tf_op jit(solution)/shard_map/reduce_scatter | solution.py:35
  87.9 74.8 %slice-start = ((s8[5308416]{0:T(1024)(128)(4,1)}), s8[1114112]{0:T(1024)(128)(4,1)S(1)}, s32[]{:S(2)}) async-start(s8[5308416]{0:T(1024)(128)(4,1)} %bitcast.30), calls=%async_computation.5 | async-start | bytes 2228224
  158.7 4.0 %slice-start.1 = ((s8[5308416]{0:T(1024)(128)(4,1)}), s8[4194304]{0:T(1024)(128)(4,1)S(1)}, s32[]{:S(2)}) async-start(s8[5308416]{0:T(1024)(128)(4,1)} %bitcast.30), calls=%async_computation.6 | async-start | bytes 8388608
  162.7 2.5 copy-start.1
  212.7 4.7 %copy-start = (f32[1152,1152]{1,0:T(8,128)S(1)}, f32[1152,1152]{1,0:T(8,128)}, u32[]{:S(2)}) copy-start(f32[1152,1152]{1,0:T(8,128)} %get-tuple-element.114) | copy-start | bytes 15925252
Sparse Core Ops, SparseCore 0:
  9.5 78.3 all-gather.4
  89.4 69.2 all-gather.2
  168.0 54.0 reduce-scatter.3
where the time goes:
time: 267 us; the launch traced here: 266 us
  waiting for transfers between devices  135 us (51%)
  blocking collectives  61.8 us (23%)
  other arithmetic  27.3 us (10%)
  matrix products  21.2 us (8%)
  between operations  13.9 us (5%)
  starting transfers between devices  3.64 us (1%)
  local copies, waits for them, and re-layouts  3.38 us (1%)
    all_gather x1, waiting for transfers between devices, shards(): lax.all_gather(w_up, 'dp', axis=0, tiled=True)  67.1 us
    all_gather x1, waiting for transfers between devices, shards(): lax.all_gather(w_gate, 'dp', axis=0, tiled=True)  63.6 us
    psum x1, blocking collectives, shards(): row_sum = lax.psum(row_part, ('tp', 'section'))  29.5 us
    add x2, other arithmetic, one_block(): total + lax.optimization_barrier(term.astype(jnp.bfloat16)).astype(jnp.fl...  16.6 us
    all_gather x1, blocking collectives, shards(): piece_up = lax.all_gather(d_up, 'dp', axis=0, tiled=True)  9.34 us
    all_gather x1, blocking collectives, shards(): rows_in = lax.all_gather(tokens, 'section', axis=1, tiled=True)  9.03 us
    all_gather x1, blocking collectives, shards(): piece_gate = lax.all_gather(d_gate, 'dp', axis=0, tiled=True)  8.47 us
    dot_general x2, matrix products, one_block(): lax.dot_general(block_normed, block_gate, contract_rows, preferred_elemen...  6.71 us
  transfers between devices with their start and end apart: 4, of which 3 were waited for; matrix products, arithmetic and copies ran while one was open for 18% of the time, Pallas kernels for 0%

commit v1 on v0

--- a/solution.py
+++ b/solution.py
@@ -5,6 +5,12 @@
 
 D = 2304
 epsilon = 1e-06
+
+
+def summed_here(x, mesh_axis):
+    pieces = lax.all_gather(x, mesh_axis, axis=0, tiled=False)
+    summed = pieces.sum(axis=0)
+    return summed
 
 
 def gated_unit(gate, up):
@@ -42,7 +48,7 @@
     gain_part = jnp.sum(d_normed * own_inputs * inv_rms[:, None], axis=0)
     row_part = jnp.sum(own_inputs * own_gain * d_normed, axis=1)
     grad_gain = lax.psum(gain_part, "dp")
-    row_sum = lax.psum(row_part, ("tp", "section"))
+    row_sum = summed_here(row_part, ("tp", "section"))
     grad_tokens = (
         inv_rms[:, None] * own_gain * d_normed - own_inputs * (inv_rms**3 * row_sum / D)[:, None]
     )

time: 267 us -> 257 us (0.963)
  blocking collectives: 61.8 us -> 51.7 us
    psum x1 -> x0, blocking collectives: 29.5 us -> none  [shards(): row_sum = lax.psum(row_part, ('tp', 'section'))]
    all_gather x0 -> x1, blocking collectives: none -> 19.4 us  [summed_here(): pieces = lax.all_gather(x, mesh_axis, axis=0, tiled=False)]
  transfers between devices with their start and end apart: 4 -> 4, of which waited for: 3 -> 3; matrix products, arithmetic and copies ran while one was open for 18% -> 19% of each run, Pallas kernels for 0% -> 0%
where the time goes in v1:
time: 257 us; the launch traced here: 256 us
  waiting for transfers between devices  135 us (53%)
  blocking collectives  51.7 us (20%)
  other arithmetic  27.3 us (11%)
  matrix products  21.2 us (8%)
  between operations  13.9 us (5%)
  starting transfers between devices  3.64 us (1%)
  local copies, waits for them, and re-layouts  3.38 us (1%)
    all_gather x1, waiting for transfers between devices, shards(): lax.all_gather(w_up, 'dp', axis=0, tiled=True)  67.1 us
    all_gather x1, waiting for transfers between devices, shards(): lax.all_gather(w_gate, 'dp', axis=0, tiled=True)  63.6 us
    all_gather x1, blocking collectives, summed_here(): pieces = lax.all_gather(x, mesh_axis, axis=0, tiled=False)  19.4 us
    add x2, other arithmetic, one_block(): total + lax.optimization_barrier(term.astype(jnp.bfloat16)).astype(jnp.fl...  16.6 us
    all_gather x1, blocking collectives, shards(): piece_up = lax.all_gather(d_up, 'dp', axis=0, tiled=True)  9.34 us
    all_gather x1, blocking collectives, shards(): rows_in = lax.all_gather(tokens, 'section', axis=1, tiled=True)  9.03 us
    all_gather x1, blocking collectives, shards(): piece_gate = lax.all_gather(d_gate, 'dp', axis=0, tiled=True)  8.47 us
    dot_general x2, matrix products, one_block(): lax.dot_general(block_normed, block_gate, contract_rows, preferred_elemen...  6.71 us
  transfers between devices with their start and end apart: 4, of which 3 were waited for; matrix products, arithmetic and copies ran while one was open for 19% of the time, Pallas kernels for 0%

profile of v1, /device:TPU:0, one launch (start us, length us, event | category | flops | bytes accessed | tf_op | source)
XLA Modules:
  0.0 256.2 jit_solution(18416864660479428824)
XLA Ops:
  7.2 0.0 copy-start.3
  7.2 0.0 copy-start.4
  7.2 0.0 all-gather.7.cloned.1.call-start
  7.2 0.7 all-gather.7.cloned.1.call-update
  7.9 0.0 copy-start.2
  7.9 0.0 all-gather.5.cloned.1.call-start
  8.0 0.7 all-gather.5.cloned.1.call-update
  8.7 0.0 copy-done.3
  8.7 9.0 %all_gather.21 = bf16[128,2304]{0,1:T(8,128)(2,1)S(1)} all-gather(bf16[128,576]{0,1:T(8,128)(2,1)S(1)} %copy-done.3), channel_id=1, replica_groups=mesh['dp'=2,'tp'=4,'section'=4] {'section'}, dimensions={1}, use_global_device_ids=true | all-gather | bytes 737280 | tf_op jit(solution)/shard_map/all_gather | solution.py:21
  17.7 0.3 multiply_reduce_fusion
  18.1 0.0 copy-done.4
  18.1 0.4 multiply_convert_fusion
  18.4 1.1 copy.13
  19.5 3.5 %all-to-all-start = ((bf16[128,2,1152]{2,0,1:T(8,128)(2,1)}), bf16[128,2,1152]{2,0,1:T(8,128)(2,1)S(1)}, u32[]{:S(2)}, u32[]{:S(2)}) async-start(bf16[128,2,1152]{2,0,1:T(8,128)(2,1)} %copy.13), calls=%async_computation | async-start | bytes 1179648 | tf_op jit(solution)/shard_map/all_to_all | solution.py:57
  23.0 0.0 reduce-scatter.4.cloned.1.call-start
  23.1 1.1 convert_element_type.59
  24.2 0.1 dynamic_slice.27
  24.3 63.6 %all-gather.7.cloned.1.call-done = bf16[2304,1152]{1,0:T(8,128)(2,1)} async-done(((bf16[1152,1152]{1,0:T(8,128)(2,1)}), bf16[2304,1152]{1,0:T(8,128)(2,1)}) %all-gather.7.cloned.1.call-update) | async-done | bytes 5308432 | tf_op jit(solution)/shard_map/all_gather | solution.py:26
  87.9 0.0 copy-done.2
  87.9 3.7 %fusion.8 = (bf16[128,1152]{1,0:T(8,128)(2,1)S(1)}, f32[128,1152]{1,0:T(8,128)S(1)}) fusion(bf16[128,1152]{1,0:T(8,128)(2,1)S(1)} %copy-done.2, bf16[128,2304]{0,1:T(8,128)(2,1)S(1)} %multiply_convert_fusion, bf16[2304,1152]{1,0:T(8,128)(2,1)} %all-gather.7.cloned.1.call-done), kind=kOutput, calls=%fused_computation.19 | convolution fusion | flops 681099264 | bytes 7077888 | tf_op jit(solution)/shard_map/dot_general | solution.py:29
  91.6 67.1 %all-gather.5.cloned.1.call-done = bf16[2304,1152]{1,0:T(8,128)(2,1)} async-done(((bf16[1152,1152]{1,0:T(8,128)(2,1)}), bf16[2304,1152]{1,0:T(8,128)(2,1)}) %all-gather.5.cloned.1.call-update) | async-done | bytes 5308432 | tf_op jit(solution)/shard_map/all_gather | solution.py:27
  158.7 4.0 %fusion.15 = bf16[128,1152]{1,0:T(8,128)(2,1)S(1)} fusion(f32[128,1152]{1,0:T(8,128)S(1)} %get-tuple-element.158, bf16[128,2304]{0,1:T(8,128)(2,1)S(1)} %multiply_convert_fusion, bf16[2304,1152]{1,0:T(8,128)(2,1)} %all-gather.5.cloned.1.call-done, bf16[128,1152]{1,0:T(8,128)(2,1)} %param.8), kind=kOutput, calls=%fused_computation.26 | convolution fusion | flops 682721280 | bytes 7077888 | tf_op jit(solution)/shard_map/dot_general | solution.py:30
  162.7 0.0 slice-done
  162.7 0.0 slice-done.1
  162.7 0.0 copy-start.1
  162.7 1.6 fusion.23
  164.3 0.9 copy-done.1
  165.2 1.6 fusion.7
  166.8 1.1 copy.14
  167.9 0.0 reduce-scatter.4.cloned.1.call-update
  167.9 9.3 %all_gather.27 = bf16[256,1152]{1,0:T(8,128)(2,1)} all-gather(bf16[128,1152]{1,0:T(8,128)(2,1)S(1)} %get-tuple-element.157), channel_id=1, replica_groups=mesh['dp'=2,'tp'=4,'section'=4] {'dp'}, dimensions={0}, use_global_device_ids=true | all-gather | bytes 884736 | tf_op jit(solution)/shard_map/all_gather | solution.py:61
  177.2 8.5 %all_gather.26 = bf16[256,1152]{1,0:T(8,128)(2,1)} all-gather(bf16[128,1152]{1,0:T(8,128)(2,1)S(1)} %fusion.15), channel_id=1, replica_groups=mesh['dp'=2,'tp'=4,'section'=4] {'dp'}, dimensions={0}, use_global_device_ids=true | all-gather | bytes 884736 | tf_op jit(solution)/shard_map/all_gather | solution.py:60
  185.7 0.0 all-to-all-done
  185.7 27.0 %while.16 = (s32[]{:T(128)}, f32[1152,1152]{1,0:T(8,128)}, f32[1152,1152]{1,0:T(8,128)}, bf16[256,1152]{1,0:T(8,128)(2,1)S(1)}, bf16[256,1152]{1,0:T(8,128)(2,1)...) while((s32[]{:T(128)}, f32[1152,1152]{1,0:T(8,128)}, ...), condition=%wide.region_7.0_spmd.clone, body=%wide.region_6.0_spmd.clone.sunk | while | flops 690094080 | bytes 33032356 | solution.py:83
  185.7 1.8 convolution_convert_fusion.4
  187.6 3.4 %convolution_convert_fusion.5 = bf16[1152,1152]{1,0:T(8,128)(2,1)} fusion(bf16[256,1152]{1,0:T(8,128)(2,1)} %get-tuple-element.224, s32[]{:T(128)S(6)} %select_n.16, bf16[256,1152]{1,0:T(8,128)(2,1)S(1)} %get-tuple-element.223), kind=kOutput, calls=%fused_computation.1.clone.1 | convolution fusion | flops 341065728 | bytes 3245056 | tf_op jit(solution)/shard_map/while/body/eval_jaxpr/dot_general | solution.py:69
  190.9 6.7 %select_add_fusion.3 = (f32[1152,1152]{1,0:T(8,128)}, f32[1152,1152]{1,0:T(8,128)}) fusion(f32[1152,1152]{1,0:T(8,128)} %get-tuple-element.212, bf16[1152,1152]{1,0:T(8,128)(2,1)S(1)} %convolution_convert_fusion.4, pred[]{:T(512)S(6)} %compare.3, bf16[1152,1152]{1,0:T(8,128)(2,1)} %convolution_convert_fusion.5, f32[1152,1152]{1,0:T(8,128)} %get-tuple-element.211), kind=kLoop, calls=%fused_computation.2.clone.1 | loop fusion | flops 7962624 | bytes 26542080 | tf_op jit(solution)/shard_map/while/body/eval_jaxpr/add | solution.py:78
  197.6 1.8 convolution_convert_fusion.4
  199.5 3.4 %convolution_convert_fusion.5 = bf16[1152,1152]{1,0:T(8,128)(2,1)} fusion(bf16[256,1152]{1,0:T(8,128)(2,1)} %get-tuple-element.224, s32[]{:T(128)S(6)} %select_n.16, bf16[256,1152]{1,0:T(8,128)(2,1)S(1)} %get-tuple-element.223), kind=kOutput, calls=%fused_computation.1.clone.1 | convolution fusion | flops 341065728 | bytes 3245056 | tf_op jit(solution)/shard_map/while/body/eval_jaxpr/dot_general | solution.py:69
  202.8 9.9 %select_add_fusion.3 = (f32[1152,1152]{1,0:T(8,128)}, f32[1152,1152]{1,0:T(8,128)}) fusion(f32[1152,1152]{1,0:T(8,128)} %get-tuple-element.212, bf16[1152,1152]{1,0:T(8,128)(2,1)S(1)} %convolution_convert_fusion.4, pred[]{:T(512)S(6)} %compare.3, bf16[1152,1152]{1,0:T(8,128)(2,1)} %convolution_convert_fusion.5, f32[1152,1152]{1,0:T(8,128)} %get-tuple-element.211), kind=kLoop, calls=%fused_computation.2.clone.1 | loop fusion | flops 7962624 | bytes 26542080 | tf_op jit(solution)/shard_map/while/body/eval_jaxpr/add | solution.py:78
  212.7 4.4 %convert_element_type.68 = bf16[1152,1152]{1,0:T(8,128)(2,1)} convert(f32[1152,1152]{1,0:T(8,128)} %get-tuple-element.115) | non-fusion elementwise | flops 1327104 | bytes 7962624 | tf_op jit(solution)/shard_map/convert_element_type | solution.py:90
  217.1 0.2 copy-done
  217.3 1.8 convert_element_type.67
  219.1 3.0 %reduce-scatter.4.cloned.1.call-done = bf16[144,128]{1,0:T(8,128)(2,1)} async-done(((bf16[2304,128]{1,0:T(8,128)(2,1)}), bf16[144,128]{1,0:T(8,128)(2,1)}) %reduce-scatter.4.cloned.1.call-update) | async-done | bytes 36880 | tf_op jit(solution)/shard_map/reduce_scatter | solution.py:41
  222.1 1.1 fusion.20
  223.2 5.5 %psum.7 = f32[144]{0:T(256)} all-reduce(f32[144]{0:T(256)S(1)} %get-tuple-element.141), channel_id=1, replica_groups=mesh['dp'=2,'tp'=4,'section'=4] {'dp'}, use_global_device_ids=true, to_apply=%region_5.0 | all-reduce | flops 144 | bytes 1152 | tf_op jit(solution)/shard_map/psum | solution.py:50
  228.6 19.4 %all-gather.1 = f32[16,1,128]{2,1,0:T(1,128)S(1)} all-gather(f32[1,1,128]{2,1,0:T(1,128)S(1)} %bitcast.34), channel_id=2, replica_groups=mesh['dp'=2,'tp'=4,'section'=4] {'tp','section'}, dimensions={0}, use_global_device_ids=true | all-gather | bytes 8704 | tf_op jit(solution)/shard_map/all_gather | solution.py:11
  248.1 1.6 fusion.17
  (9 shorter events, 0.1 us)
Async XLA Ops:
  7.2 1.5 copy-start.3
  7.2 10.9 %copy-start.4 = (f32[2304]{0:T(1024)S(1)}, f32[2304]{0:T(1024)}, u32[]{:S(2)}) copy-start(f32[2304]{0:T(1024)} %param.9) | copy-start | bytes 27652
  7.2 80.7 %all-gather.7.cloned.1.call-start = ((), (), s32[]{:S(2)}) async-start(), calls=%async_computation.3 | async-start | bytes 7962624 | tf_op jit(solution)/shard_map/all_gather | solution.py:26
  7.9 80.0 %copy-start.2 = (bf16[128,1152]{1,0:T(8,128)(2,1)S(1)}, bf16[128,1152]{1,0:T(8,128)(2,1)}, u32[]{:S(2)}) copy-start(bf16[128,1152]{1,0:T(8,128)(2,1)} %param.8) | copy-start | bytes 884740
  7.9 150.8 %all-gather.5.cloned.1.call-start = ((), (), s32[]{:S(2)}) async-start(), calls=%async_computation.2 | async-start | bytes 7962624 | tf_op jit(solution)/shard_map/all_gather | solution.py:27
  19.5 166.2 %all-to-all-start = ((bf16[128,2,1152]{2,0,1:T(8,128)(2,1)}), bf16[128,2,1152]{2,0,1:T(8,128)(2,1)S(1)}, u32[]{:S(2)}, u32[]{:S(2)}) async-start(bf16[128,2,1152]{2,0,1:T(8,128)(2,1)} %copy.13), calls=%async_computation | async-start | bytes 1179648 | tf_op jit(solution)/shard_map/all_to_all | solution.py:57
  23.0 199.1 %reduce-scatter.4.cloned.1.call-start = ((), (), s32[]{:S(2)}) async-start(), calls=%async_computation.4 | async-start | bytes 626688 | tf_op jit(solution)/shard_map/reduce_scatter | solution.py:41
  87.9 74.8 %slice-start = ((s8[5308416]{0:T(1024)(128)(4,1)}), s8[1114112]{0:T(1024)(128)(4,1)S(1)}, s32[]{:S(2)}) async-start(s8[5308416]{0:T(1024)(128)(4,1)} %bitcast.31), calls=%async_computation.5 | async-start | bytes 2228224
  158.7 4.0 %slice-start.1 = ((s8[5308416]{0:T(1024)(128)(4,1)}), s8[4194304]{0:T(1024)(128)(4,1)S(1)}, s32[]{:S(2)}) async-start(s8[5308416]{0:T(1024)(128)(4,1)} %bitcast.31), calls=%async_computation.6 | async-start | bytes 8388608
  162.7 2.5 copy-start.1
  212.7 4.7 %copy-start = (f32[1152,1152]{1,0:T(8,128)S(1)}, f32[1152,1152]{1,0:T(8,128)}, u32[]{:S(2)}) copy-start(f32[1152,1152]{1,0:T(8,128)} %get-tuple-element.114) | copy-start | bytes 15925252
Sparse Core Ops, SparseCore 0:
  9.5 78.3 all-gather.6
  89.4 69.2 all-gather.4
  168.0 54.0 reduce-scatter.3
